TPU v7x, 128 devices: a whole 4x4x4 slice. The times are simulated.
128 devices in a mesh: island: 8 (over x_lo, z), shard: 16 (over y, x_hi, core).
Axes of the slice: x: 4 (x_hi: 2, x_lo: 2; x = x_hi * 2 + x_lo), y: 4, z: 4, core: 2. Of those that a mesh axis runs over, the one named last changes fastest.
Arguments:
- weight_master: float32 [4096, 4096], P('island', 'shard'), may hold values from -6 to 6
- gain_master: float32 [4096], P(('shard', 'island')), may hold values from 0.5 to 1.5
- weight_moment: float32 [4096, 4096], P('island', 'shard'), may hold values from -0.3 to 0.3
- gain_moment: float32 [4096], P(('shard', 'island')), may hold values from -0.3 to 0.3
- attended: bfloat16 [8, 2, 1536, 4096], P('island', None, 'shard'), may hold values from -6 to 6
- stream: bfloat16 [8, 2, 1536, 4096], P('island', None, None, 'shard'), may hold values from -6 to 6
- targets: bfloat16 [8, 2, 1536, 4096], P('island', None, None, 'shard'), may hold values from -6 to 6
Outputs:
- weight_updated: float32 [4096, 4096], P('island', 'shard')
- gain_updated: float32 [4096], P(('shard', 'island'))
- weight_velocity: float32 [4096, 4096], P('island', 'shard')
- gain_velocity: float32 [4096], P(('shard', 'island'))
All inputs are finite; a program needn't handle non-finite values.
Results may differ from a plain program's by a relative error of at most 0.0066.
Values may be sent and summed in bfloat16 or wider, within the bound.
No kernel may reach another device: no remote copies, remote signals or barrier semaphores. Data moves between devices by JAX's collectives and lax.ppermute only.
A program may use at most 192 MiB of HBM per device.

v0:
```python
import jax
import jax.numpy as jnp
from jax import lax
from jax.sharding import Mesh
from jax.sharding import PartitionSpec as P

D = 4096
STEPS = 2
SHARD = ("shard_0", "shard_1", "shard_2")
SHARD_ISLAND = ("shard_0", "shard_1", "shard_2", "island")
norm_epsilon = 1e-05
inner_rate = 0.05
beta_one = 0.9
beta_two = 0.95
adam_epsilon = 0.3
decay_rate = 0.1
outer_rate = 0.7
outer_momentum = 0.9


def joined_along(blocks, dim):
    shape = list(blocks.shape[1:])
    shape[dim] *= blocks.shape[0]
    return jnp.moveaxis(blocks, 0, dim).reshape(shape)


def gather_packed(arrays, axis, dims):
    vector = jnp.concatenate([a.reshape(-1) for a in arrays])
    lines, at, gathered = (lax.all_gather(vector, axis), 0, [])
    for a, dim in zip(arrays, dims):
        blocks = lines[:, at : at + a.size].reshape(-1, *a.shape)
        gathered.append(joined_along(blocks, dim))
        at += a.size
    return tuple(gathered)


def one_axis_at_a_time(value, axes):
    for axis in axes:
        value = lax.psum(value, axis)
    return value


def copy_for_each(value, axis):
    copies = jnp.broadcast_to(value, (lax.axis_size(axis), *value.shape))
    return lax.all_to_all(copies, axis, split_axis=0, concat_axis=0, tiled=True)


def taken_together(value, axis):
    everything = copy_for_each(value, axis)
    return jnp.sum(everything, axis=0)


def split_up(value, dim, size):
    shape = value.shape
    blocks = value.reshape(*shape[:dim], size, shape[dim] // size, *shape[dim + 1 :])
    return jnp.moveaxis(blocks, dim, 0)


def sent_and_summed(value, axis, dim):
    blocks = split_up(value, dim, lax.axis_size(axis))
    arrived = lax.all_to_all(blocks, axis, split_axis=0, concat_axis=0, tiled=True)
    return arrived.astype(jnp.float32).sum(axis=0)


def optimizer_update(param, gradient, first, second, number, decay):
    first = beta_one * first + (1.0 - beta_one) * gradient
    second = beta_two * second + (1.0 - beta_two) * gradient * gradient
    first_hat = first / (1.0 - beta_one**number)
    second_hat = second / (1.0 - beta_two**number)
    param = param - inner_rate * (first_hat / (jnp.sqrt(second_hat) + adam_epsilon) + decay * param)
    return (param, first, second)


def per_device(weight_master, gain_master, weight_moment, gain_moment, attended, stream, targets):
    islands = lax.axis_size("island")
    width_scale = D ** (-0.5)
    starts = gather_packed(
        (weight_master.astype(jnp.bfloat16), gain_master.astype(jnp.bfloat16)), "island", (0, 0)
    )
    weight_anchor = starts[0].astype(jnp.float32)
    gain_anchor = starts[1].astype(jnp.float32)
    weight = weight_anchor
    gain = gain_anchor
    weight_first = jnp.zeros_like(weight)
    weight_second = jnp.zeros_like(weight)
    gain_first = jnp.zeros_like(gain)
    gain_second = jnp.zeros_like(gain)
    for inner_step in range(STEPS):
        number = inner_step + 1
        rows_full = lax.all_gather(attended[0][inner_step], SHARD, axis=0, tiled=True)
        weight_low = weight.astype(jnp.bfloat16)
        projected = jnp.dot(rows_full, weight_low, preferred_element_type=jnp.float32) * width_scale
        residual = stream[0][inner_step].astype(jnp.float32) + projected
        squares = one_axis_at_a_time(jnp.sum(residual * residual, axis=1), SHARD)
        inverse = lax.rsqrt(squares / D + norm_epsilon)[:, None]
        normed = residual * inverse * gain
        loss_low = (normed - targets[0][inner_step].astype(jnp.float32)).astype(jnp.bfloat16)
        loss_grad = lax.optimization_barrier(loss_low).astype(jnp.float32)
        scaled = loss_grad * gain
        slope = taken_together(jnp.sum(scaled * residual, axis=1), SHARD)[:, None]
        residual_grad = (
            inverse * scaled - residual * inverse * inverse * inverse * slope / D
        ).astype(jnp.bfloat16)
        weight_grad = (
            jnp.einsum("td,tf->df", rows_full, residual_grad, preferred_element_type=jnp.float32)
            * width_scale
        )
        gain_grad = jnp.sum(loss_grad * residual * inverse, axis=0)
        weight, weight_first, weight_second = optimizer_update(
            weight, weight_grad, weight_first, weight_second, number, decay_rate
        )
        gain, gain_first, gain_second = optimizer_update(
            gain, gain_grad, gain_first, gain_second, number, 0.0
        )
    weight_summed, gain_summed = (
        sent_and_summed((weight_anchor - weight).astype(jnp.bfloat16), "island", 0),
        sent_and_summed((gain_anchor - gain).astype(jnp.bfloat16), "island", 0),
    )
    weight_pseudo = weight_summed / islands
    gain_pseudo = gain_summed / islands
    weight_velocity = outer_momentum * weight_moment + weight_pseudo
    gain_velocity = outer_momentum * gain_moment + gain_pseudo
    weight_updated = weight_master - outer_rate * (weight_pseudo + outer_momentum * weight_velocity)
    gain_updated = gain_master - outer_rate * (gain_pseudo + outer_momentum * gain_velocity)
    return (weight_updated, gain_updated, weight_velocity, gain_velocity)


def solution(mesh):
    torus = Mesh(
        mesh.devices.reshape(mesh.shape["island"], 4, 2, 2),
        ("island", "shard_0", "shard_1", "shard_2"),
    )
    return jax.shard_map(
        per_device,
        mesh=torus,
        in_specs=(
            P("island", SHARD),
            P(SHARD_ISLAND),
            P("island", SHARD),
            P(SHARD_ISLAND),
            P("island", None, SHARD, None),
            P("island", None, None, SHARD),
            P("island", None, None, SHARD),
        ),
        out_specs=(P("island", SHARD), P(SHARD_ISLAND), P("island", SHARD), P(SHARD_ISLAND)),
        check_vma=False,
    )
```

profile of v0, /device:TPU:1, one launch (start us, length us, event | category | flops | bytes accessed | tf_op | source)
XLA Modules:
  0.0 327.8 jit_solution(17486455540308748270)
XLA Ops:
  12.1 2.6 dynamic-update-slice
  16.2 2.8 fusion.91
  24.9 119.6 %all-reduce.3.cloned.1.call-done = bf16[1048832]{0:T(1024)(128)(2,1)} async-done(((bf16[1048832]{0:T(1024)(128)(2,1)}), bf16[1048832]{0:T(1024)(128)(2,1)}) %all-reduce.3.cloned.1.call-update) | async-done | bytes 2097680
  144.5 4.1 %reshape.82 = bf16[8,131104]{1,0:T(8,128)(2,1)S(1)} reshape(bf16[1048832]{0:T(1024)(128)(2,1)} %all-reduce.3.cloned.1.call-done) | data formatting | bytes 4195328 | tf_op jit(solution)/shard_map/all_gather | solution.py:29
  150.0 3.9 %reshape_reshape.3 = bf16[4096,256]{1,0:T(8,128)(2,1)} reshape(bf16[8,131072]{1,0:T(8,128)(2,1)} %slice.38) | data formatting | bytes 4194304 | tf_op jit(solution)/shard_map/reshape;reshape | solution.py:24
  154.0 4.2 %copy.55 = bf16[4096,256]{0,1:T(8,128)(2,1)} copy(bf16[4096,256]{1,0:T(8,128)(2,1)} %reshape_reshape.3) | data formatting | bytes 4194304 | tf_op jit(solution)/shard_map/reshape;reshape | solution.py:24
  158.2 10.2 %multiply_reduce_fusion.1 = (f32[1536]{0:T(1024)S(1)}, f32[1536,256]{0,1:T(8,128)}) fusion(bf16[4096,256]{1,0:T(8,128)(2,1)} %reshape_reshape.3, bf16[1,1,1536,4096]{3,2,1,0:T(8,128)(2,1)} %all-gather.6.cloned.1.call-done, bf16[1,1,1536,256]{2,3,1,0:T(8,128)(2,1)} %copy.72), kind=kOutput, calls=%fused_computation.56 | convolution fusion | flops 3223190016 | bytes 17045504 | tf_op jit(solution)/shard_map/dot_general | solution.py:92
  168.5 9.4 %psum.42 = f32[1536]{0:T(1024)S(1)} all-reduce(f32[1536]{0:T(1024)S(1)} %get-tuple-element.34), channel_id=1, replica_groups=mesh['island'=8,'shard_0'=4,'shard_1'=2,'shard_2'=2] {'shard_0'}, use_global_device_ids=true, to_apply=%region_1.0 | all-reduce | flops 1536 | bytes 12288 | tf_op jit(solution)/shard_map/psum | solution.py:39
  177.9 6.0 %psum.43 = f32[1536]{0:T(1024)S(1)} all-reduce(f32[1536]{0:T(1024)S(1)} %psum.42), channel_id=1, replica_groups=mesh['island'=8,'shard_0'=4,'shard_1'=2,'shard_2'=2] {'shard_1'}, use_global_device_ids=true, to_apply=%region_2.0 | all-reduce | flops 1536 | bytes 12288 | tf_op jit(solution)/shard_map/psum | solution.py:39
  183.9 9.4 %psum.44 = f32[1536]{0:T(1024)S(1)} all-reduce(f32[1536]{0:T(1024)S(1)} %psum.43), channel_id=1, replica_groups=mesh['island'=8,'shard_0'=4,'shard_1'=2,'shard_2'=2] {'shard_2'}, use_global_device_ids=true, to_apply=%region_3.0 | all-reduce | flops 1536 | bytes 12288 | tf_op jit(solution)/shard_map/psum | solution.py:39
  193.4 2.0 fusion.54
  197.1 4.8 %all-to-all-start = ((f32[16,1,1536]{2,1,0:T(1,128)}), f32[16,1,1536]{2,1,0:T(1,128)S(1)}, u32[]{:S(2)}, u32[]{:S(2)}) async-start(f32[16,1,1536]{2,1,0:T(1,128)} %broadcast_in_dim.4), calls=%async_computation | async-start | bytes 196608 | tf_op jit(solution)/shard_map/all_to_all | solution.py:45
  201.9 7.2 %all-to-all-done = f32[16,1,1536]{2,1,0:T(1,128)S(1)} async-done(((f32[16,1,1536]{2,1,0:T(1,128)}), f32[16,1,1536]{2,1,0:T(1,128)S(1)}, u32[]{:S(2)}, u32[]{:S(2)}) %all-to-all-start) | async-done | bytes 98336 | tf_op jit(solution)/shard_map/all_to_all | solution.py:45
  209.3 10.9 %fusion.4 = f32[256,4096]{1,0:T(8,128)} fusion(bf16[1,1,1536,4096]{3,2,1,0:T(8,128)(2,1)} %all-gather.6.cloned.1.call-done, bf16[1536,256]{0,1:T(8,128)(2,1)} %copy-done.4, f32[1536,256]{0,1:T(8,128)} %get-tuple-element.35, f32[1536]{0:T(1024)S(1)} %reduce_sum.96, f32[256]{0:T(256)S(1)} %reshape.78, f32[1536]{0:T(1024)S(1)} %add_rsqrt_fusion.1), kind=kOutput, calls=%fused_computation.4 | convolution fusion | flops 3225157632 | bytes 19149824 | tf_op jit(solution)/shard_map/td,tf->df/dot_general | solution.py:105
  220.2 13.4 %multiply_reduce_fusion = (f32[1536]{0:T(1024)S(1)}, f32[1536,256]{0,1:T(8,128)}) fusion(bf16[1,1,1536,4096]{3,2,1,0:T(8,128)(2,1)} %all-gather.8.cloned.1.call-done, f32[256,4096]{1,0:T(8,128)} %fusion.4, bf16[4096,256]{0,1:T(8,128)(2,1)} %copy.55, bf16[1,1,1536,256]{2,3,1,0:T(8,128)(2,1)} %copy.74), kind=kOutput, calls=%fused_computation.55 | convolution fusion | flops 3235772928 | bytes 21239808 | tf_op jit(solution)/shard_map/dot_general | solution.py:92
  233.6 7.0 %psum.45 = f32[1536]{0:T(1024)S(1)} all-reduce(f32[1536]{0:T(1024)S(1)} %get-tuple-element.36), channel_id=1, replica_groups=mesh['island'=8,'shard_0'=4,'shard_1'=2,'shard_2'=2] {'shard_0'}, use_global_device_ids=true, to_apply=%region_7.0 | all-reduce | flops 1536 | bytes 12288 | tf_op jit(solution)/shard_map/psum | solution.py:39
  240.6 5.4 %psum.46 = f32[1536]{0:T(1024)S(1)} all-reduce(f32[1536]{0:T(1024)S(1)} %psum.45), channel_id=1, replica_groups=mesh['island'=8,'shard_0'=4,'shard_1'=2,'shard_2'=2] {'shard_1'}, use_global_device_ids=true, to_apply=%region_8.0 | all-reduce | flops 1536 | bytes 12288 | tf_op jit(solution)/shard_map/psum | solution.py:39
  246.0 5.7 %psum.47 = f32[1536]{0:T(1024)S(1)} all-reduce(f32[1536]{0:T(1024)S(1)} %psum.46), channel_id=1, replica_groups=mesh['island'=8,'shard_0'=4,'shard_1'=2,'shard_2'=2] {'shard_2'}, use_global_device_ids=true, to_apply=%region_9.0 | all-reduce | flops 1536 | bytes 12288 | tf_op jit(solution)/shard_map/psum | solution.py:39
  255.2 3.6 %all-to-all-start.1 = ((f32[16,1,1536]{2,1,0:T(1,128)}), f32[16,1,1536]{2,1,0:T(1,128)S(1)}, u32[]{:S(2)}, u32[]{:S(2)}) async-start(f32[16,1,1536]{2,1,0:T(1,128)} %broadcast_in_dim.5), calls=%async_computation.1 | async-start | bytes 196608 | tf_op jit(solution)/shard_map/all_to_all | solution.py:45
  259.4 6.8 %all-to-all-done.1 = f32[16,1,1536]{2,1,0:T(1,128)S(1)} async-done(((f32[16,1,1536]{2,1,0:T(1,128)}), f32[16,1,1536]{2,1,0:T(1,128)S(1)}, u32[]{:S(2)}, u32[]{:S(2)}) %all-to-all-start.1) | async-done | bytes 98336 | tf_op jit(solution)/shard_map/all_to_all | solution.py:45
  266.2 4.3 %all-to-all-start.3 = ((bf16[8,1,32]{2,1,0:T(2,128)(2,1)}), bf16[8,1,32]{2,1,0:T(2,128)(2,1)S(1)}, u32[]{:S(2)}, u32[]{:S(2)}) async-start(bf16[8,1,32]{2,1,0:T(2,128)(2,1)} %copy.66), calls=%async_computation.3 | async-start | bytes 8192 | tf_op jit(solution)/shard_map/all_to_all | solution.py:61
  270.6 14.3 %fusion.10 = bf16[4096,256]{0,1:T(8,128)(2,1)S(1)} fusion(bf16[4096,256]{0,1:T(8,128)(2,1)} %copy.55, f32[256,4096]{1,0:T(8,128)} %fusion.4, bf16[1,1,1536,4096]{3,2,1,0:T(8,128)(2,1)} %all-gather.8.cloned.1.call-done, bf16[1536,256]{0,1:T(8,128)(2,1)} %copy-done.3, f32[1536,256]{0,1:T(8,128)} %get-tuple-element.37, f32[1536]{0:T(1024)S(1)} %reduce_sum.100, ...), kind=kOutput, calls=%fused_computation.13 | convolution fusion | flops 3255566336 | bytes 23344128 | tf_op jit(solution)/shard_map/td,tf->df/dot_general | solution.py:105
  286.4 5.3 %all-to-all-start.2 = ((bf16[8,512,256]{1,2,0:T(8,128)(2,1)}), bf16[8,512,256]{1,2,0:T(8,128)(2,1)S(1)}, u32[]{:S(2)}, u32[]{:S(2)}) async-start(bf16[8,512,256]{1,2,0:T(8,128)(2,1)} %bitcast.114), calls=%async_computation.2 | async-start | bytes 4194304 | tf_op jit(solution)/shard_map/all_to_all | solution.py:61
  293.7 24.2 %all-to-all-done.2 = bf16[8,512,256]{1,2,0:T(8,128)(2,1)S(1)} async-done(((bf16[8,512,256]{1,2,0:T(8,128)(2,1)}), bf16[8,512,256]{1,2,0:T(8,128)(2,1)S(1)}, u32[]{:S(2)}, u32[]{:S(2)}) %all-to-all-start.2) | async-done | bytes 2097184 | tf_op jit(solution)/shard_map/all_to_all | solution.py:61
  (65 shorter events, 24.3 us)
Async XLA Ops:
  8.0 136.5 %all-reduce.3.cloned.1.call-start = ((), (), s32[]{:S(2)}) async-start(), calls=%async_computation.6 | async-start | bytes 4198400
  14.8 1.3 copy-start
  16.1 3.5 %copy-start.6 = (bf16[1,2,1536,256]{3,2,1,0:T(8,128)(2,1)S(1)}, bf16[1,2,1536,256]{3,2,1,0:T(8,128)(2,1)}, u32[]{:S(2)}) copy-start(bf16[1,2,1536,256]{3,2,1,0:T(8,128)(2,1)} %param.12) | copy-start | bytes 4718596
  16.1 142.1 %all-gather.6.cloned.1.call-start = ((), (), s32[]{:S(2)}) async-start(), calls=%async_computation.4 | async-start | bytes 13369344 | tf_op jit(solution)/shard_map/all_gather | solution.py:90
  19.0 201.2 %all-gather.8.cloned.1.call-start = ((), (), s32[]{:S(2)}) async-start(), calls=%async_computation.5 | async-start | bytes 13369344 | tf_op jit(solution)/shard_map/all_gather | solution.py:90
  193.4 2.1 copy-start.2
  195.5 0.9 copy-start.4
  197.1 12.1 %all-to-all-start = ((f32[16,1,1536]{2,1,0:T(1,128)}), f32[16,1,1536]{2,1,0:T(1,128)S(1)}, u32[]{:S(2)}, u32[]{:S(2)}) async-start(f32[16,1,1536]{2,1,0:T(1,128)} %broadcast_in_dim.4), calls=%async_computation | async-start | bytes 196608 | tf_op jit(solution)/shard_map/all_to_all | solution.py:45
  251.6 1.9 copy-start.1
  253.5 0.9 copy-start.3
  255.2 11.0 %all-to-all-start.1 = ((f32[16,1,1536]{2,1,0:T(1,128)}), f32[16,1,1536]{2,1,0:T(1,128)S(1)}, u32[]{:S(2)}, u32[]{:S(2)}) async-start(f32[16,1,1536]{2,1,0:T(1,128)} %broadcast_in_dim.5), calls=%async_computation.1 | async-start | bytes 196608 | tf_op jit(solution)/shard_map/all_to_all | solution.py:45
  266.2 20.2 %all-to-all-start.3 = ((bf16[8,1,32]{2,1,0:T(2,128)(2,1)}), bf16[8,1,32]{2,1,0:T(2,128)(2,1)S(1)}, u32[]{:S(2)}, u32[]{:S(2)}) async-start(bf16[8,1,32]{2,1,0:T(2,128)(2,1)} %copy.66), calls=%async_computation.3 | async-start | bytes 8192 | tf_op jit(solution)/shard_map/all_to_all | solution.py:61
  286.4 5.3 %copy-start.5 = (f32[512,256]{1,0:T(8,128)S(1)}, f32[512,256]{1,0:T(8,128)}, u32[]{:S(2)}) copy-start(f32[512,256]{1,0:T(8,128)} %param.7) | copy-start | bytes 1572868
  286.4 31.5 %all-to-all-start.2 = ((bf16[8,512,256]{1,2,0:T(8,128)(2,1)}), bf16[8,512,256]{1,2,0:T(8,128)(2,1)S(1)}, u32[]{:S(2)}, u32[]{:S(2)}) async-start(bf16[8,512,256]{1,2,0:T(8,128)(2,1)} %bitcast.114), calls=%async_computation.2 | async-start | bytes 4194304 | tf_op jit(solution)/shard_map/all_to_all | solution.py:61
  291.7 1.5 copy-start.7
  291.7 1.5 copy-start.8
Sparse Core Ops, SparseCore 0:
  16.2 128.2 all-reduce.2
Sparse Core Ops, SparseCore 1:
  19.1 95.1 all-gather.5
  116.5 88.7 all-gather.7
where the time goes:
time: 329 us; the launch traced here: 328 us
  waiting for transfers between devices  158 us (48%)
  matrix products  48.9 us (15%)
  blocking collectives  42.9 us (13%)
  local copies, waits for them, and re-layouts  35.1 us (11%)
  starting transfers between devices  18.1 us (6%)
  between operations  16.3 us (5%)
  other arithmetic  8.11 us (2%)
    unnamed x4, waiting for transfers between devices  120 us
    psum x6, blocking collectives, one_axis_at_a_time(): value = lax.psum(value, axis)  42.9 us
    dot_general x2, matrix products, per_device(): jnp.einsum('td,tf->df', rows_full, residual_grad, preferred_element_type=...  25.2 us
    all_to_all x2, waiting for transfers between devices, sent_and_summed(): lax.all_to_all(blocks, axis, split_axis=0, concat_axis=0, tiled=True)  24.2 us
    dot_general x2, matrix products, per_device(): jnp.dot(rows_full, weight_low, preferred_element_type=jnp.float32)  23.7 us
    all_to_all x2, waiting for transfers between devices, copy_for_each(): return lax.all_to_all(copies, axis, split_axis=0, concat_axis=0, tiled=True)  14 us
    unnamed x30, local copies, waits for them, and re-layouts  13.4 us
    all_to_all x2, starting transfers between devices, sent_and_summed(): lax.all_to_all(blocks, axis, split_axis=0, concat_axis=0, tiled=True)  9.57 us
  transfers between devices with their start and end apart: 7, of which 4 were waited for; matrix products, arithmetic and copies ran while one was open for 20% of the time, Pallas kernels for 0%

commit v1 on v0

--- a/solution.py
+++ b/solution.py
@@ -36,7 +36,7 @@
 
 def one_axis_at_a_time(value, axes):
     for axis in axes:
-        value = lax.psum(value, axis)
+        value = jnp.sum(lax.all_gather(value, axis), axis=0)
     return value
 
 

time: 329 us -> 332 us (level)
    all_gather x0 -> x6, blocking collectives: none -> 45 us  [one_axis_at_a_time(): value = jnp.sum(lax.all_gather(value, axis), axis=0)]
    psum x6 -> x0, blocking collectives: 42.9 us -> none  [one_axis_at_a_time(): value = lax.psum(value, axis)]
    unnamed x30 -> x36, local copies, waits for them, and re-layouts: 13.4 us -> 13.4 us
where the time goes in v1:
time: 332 us
  waiting for transfers between devices  158 us (48%)
  matrix products  48.9 us (15%)
  blocking collectives  45 us (14%)
  local copies, waits for them, and re-layouts  35.1 us (11%)
  starting transfers between devices  19.5 us (6%)
  between operations  16.4 us (5%)
  other arithmetic  8.27 us (2%)
    unnamed x4, waiting for transfers between devices  120 us
    all_gather x6, blocking collectives, one_axis_at_a_time(): value = jnp.sum(lax.all_gather(value, axis), axis=0)  45 us
    dot_general x2, matrix products, per_device(): jnp.einsum('td,tf->df', rows_full, residual_grad, preferred_element_type=...  25.2 us
    all_to_all x2, waiting for transfers between devices, sent_and_summed(): lax.all_to_all(blocks, axis, split_axis=0, concat_axis=0, tiled=True)  24.2 us
    dot_general x2, matrix products, per_device(): jnp.dot(rows_full, weight_low, preferred_element_type=jnp.float32)  23.7 us
    all_to_all x2, waiting for transfers between devices, copy_for_each(): return lax.all_to_all(copies, axis, split_axis=0, concat_axis=0, tiled=True)  14 us
    unnamed x36, local copies, waits for them, and re-layouts  13.4 us
    all_to_all x2, starting transfers between devices, copy_for_each(): return lax.all_to_all(copies, axis, split_axis=0, concat_axis=0, tiled=True)  10.3 us
  transfers between devices with their start and end apart: 7, of which 4 were waited for; matrix products, arithmetic and copies ran while one was open for 20% of the time, Pallas kernels for 0%

profile of v1, /device:TPU:1, one launch (start us, length us, event | category | flops | bytes accessed | tf_op | source)
XLA Modules:
  0.0 331.6 jit_solution(10572890856269305871)
XLA Ops:
  12.1 2.6 dynamic-update-slice
  16.2 2.8 fusion.91
  24.9 119.6 %all-reduce.3.cloned.1.call-done = bf16[1048832]{0:T(1024)(128)(2,1)} async-done(((bf16[1048832]{0:T(1024)(128)(2,1)}), bf16[1048832]{0:T(1024)(128)(2,1)}) %all-reduce.3.cloned.1.call-update) | async-done | bytes 2097680
  144.5 4.1 %reshape.90 = bf16[8,131104]{1,0:T(8,128)(2,1)S(1)} reshape(bf16[1048832]{0:T(1024)(128)(2,1)} %all-reduce.3.cloned.1.call-done) | data formatting | bytes 4195328 | tf_op jit(solution)/shard_map/all_gather | solution.py:29
  150.0 3.9 %reshape_reshape.3 = bf16[4096,256]{1,0:T(8,128)(2,1)} reshape(bf16[8,131072]{1,0:T(8,128)(2,1)} %slice.38) | data formatting | bytes 4194304 | tf_op jit(solution)/shard_map/reshape;reshape | solution.py:24
  154.0 4.2 %copy.55 = bf16[4096,256]{0,1:T(8,128)(2,1)} copy(bf16[4096,256]{1,0:T(8,128)(2,1)} %reshape_reshape.3) | data formatting | bytes 4194304 | tf_op jit(solution)/shard_map/reshape;reshape | solution.py:24
  158.2 10.2 %multiply_reduce_fusion.1 = (f32[1536]{0:T(1024)S(1)}, f32[1536,256]{0,1:T(8,128)}) fusion(bf16[4096,256]{1,0:T(8,128)(2,1)} %reshape_reshape.3, bf16[1,1,1536,4096]{3,2,1,0:T(8,128)(2,1)} %all-gather.18.cloned.1.call-done, bf16[1,1,1536,256]{2,3,1,0:T(8,128)(2,1)} %copy.72), kind=kOutput, calls=%fused_computation.56 | convolution fusion | flops 3223190016 | bytes 17045504 | tf_op jit(solution)/shard_map/dot_general | solution.py:92
  168.5 10.5 %all-gather.9 = f32[4,1,1536]{2,1,0:T(1,128)S(1)} all-gather(f32[1,1,1536]{2,1,0:T(1,128)S(1)} %reshape.102), channel_id=4, replica_groups=mesh['island'=8,'shard_0'=4,'shard_1'=2,'shard_2'=2] {'shard_0'}, dimensions={0}, use_global_device_ids=true | all-gather | bytes 30720 | tf_op jit(solution)/shard_map/all_gather | solution.py:39
  179.0 5.3 %all-gather.10 = f32[2,1,1536]{2,1,0:T(1,128)S(1)} all-gather(f32[1,1,1536]{2,1,0:T(1,128)S(1)} %reshape.104), channel_id=5, replica_groups=mesh['island'=8,'shard_0'=4,'shard_1'=2,'shard_2'=2] {'shard_1'}, dimensions={0}, use_global_device_ids=true | all-gather | bytes 18432 | tf_op jit(solution)/shard_map/all_gather | solution.py:39
  184.4 9.4 %all-gather.11 = f32[2,1,1536]{2,1,0:T(1,128)S(1)} all-gather(f32[1,1,1536]{2,1,0:T(1,128)S(1)} %reshape.106), channel_id=6, replica_groups=mesh['island'=8,'shard_0'=4,'shard_1'=2,'shard_2'=2] {'shard_2'}, dimensions={0}, use_global_device_ids=true | all-gather | bytes 18432 | tf_op jit(solution)/shard_map/all_gather | solution.py:39
  193.8 2.0 fusion.54
  197.5 6.7 %all-to-all-start = ((f32[16,1,1536]{2,1,0:T(1,128)}), f32[16,1,1536]{2,1,0:T(1,128)S(1)}, u32[]{:S(2)}, u32[]{:S(2)}) async-start(f32[16,1,1536]{2,1,0:T(1,128)} %broadcast_in_dim.4), calls=%async_computation | async-start | bytes 196608 | tf_op jit(solution)/shard_map/all_to_all | solution.py:45
  204.2 7.3 %all-to-all-done = f32[16,1,1536]{2,1,0:T(1,128)S(1)} async-done(((f32[16,1,1536]{2,1,0:T(1,128)}), f32[16,1,1536]{2,1,0:T(1,128)S(1)}, u32[]{:S(2)}, u32[]{:S(2)}) %all-to-all-start) | async-done | bytes 98336 | tf_op jit(solution)/shard_map/all_to_all | solution.py:45
  211.6 10.9 %fusion.4 = f32[256,4096]{1,0:T(8,128)} fusion(bf16[1,1,1536,4096]{3,2,1,0:T(8,128)(2,1)} %all-gather.18.cloned.1.call-done, bf16[1536,256]{0,1:T(8,128)(2,1)} %copy-done.4, f32[1536,256]{0,1:T(8,128)} %get-tuple-element.35, f32[1536]{0:T(1024)S(1)} %reduce_sum.153, f32[256]{0:T(256)S(1)} %reshape.86, f32[1536]{0:T(1024)S(1)} %add_rsqrt_fusion.1), kind=kOutput, calls=%fused_computation.4 | convolution fusion | flops 3225157632 | bytes 19149824 | tf_op jit(solution)/shard_map/td,tf->df/dot_general | solution.py:105
  222.5 13.5 %multiply_reduce_fusion = (f32[1536]{0:T(1024)S(1)}, f32[1536,256]{0,1:T(8,128)}) fusion(bf16[1,1,1536,4096]{3,2,1,0:T(8,128)(2,1)} %all-gather.20.cloned.1.call-done, f32[256,4096]{1,0:T(8,128)} %fusion.4, bf16[4096,256]{0,1:T(8,128)(2,1)} %copy.55, bf16[1,1,1536,256]{2,3,1,0:T(8,128)(2,1)} %copy.74), kind=kOutput, calls=%fused_computation.55 | convolution fusion | flops 3235772928 | bytes 21239808 | tf_op jit(solution)/shard_map/dot_general | solution.py:92
  236.0 9.1 %all-gather.12 = f32[4,1,1536]{2,1,0:T(1,128)S(1)} all-gather(f32[1,1,1536]{2,1,0:T(1,128)S(1)} %reshape.108), channel_id=8, replica_groups=mesh['island'=8,'shard_0'=4,'shard_1'=2,'shard_2'=2] {'shard_0'}, dimensions={0}, use_global_device_ids=true | all-gather | bytes 30720 | tf_op jit(solution)/shard_map/all_gather | solution.py:39
  245.1 4.7 %all-gather.13 = f32[2,1,1536]{2,1,0:T(1,128)S(1)} all-gather(f32[1,1,1536]{2,1,0:T(1,128)S(1)} %reshape.110), channel_id=9, replica_groups=mesh['island'=8,'shard_0'=4,'shard_1'=2,'shard_2'=2] {'shard_1'}, dimensions={0}, use_global_device_ids=true | all-gather | bytes 18432 | tf_op jit(solution)/shard_map/all_gather | solution.py:39
  249.8 6.1 %all-gather.14 = f32[2,1,1536]{2,1,0:T(1,128)S(1)} all-gather(f32[1,1,1536]{2,1,0:T(1,128)S(1)} %reshape.112), channel_id=10, replica_groups=mesh['island'=8,'shard_0'=4,'shard_1'=2,'shard_2'=2] {'shard_2'}, dimensions={0}, use_global_device_ids=true | all-gather | bytes 18432 | tf_op jit(solution)/shard_map/all_gather | solution.py:39
  259.5 3.6 %all-to-all-start.1 = ((f32[16,1,1536]{2,1,0:T(1,128)}), f32[16,1,1536]{2,1,0:T(1,128)S(1)}, u32[]{:S(2)}, u32[]{:S(2)}) async-start(f32[16,1,1536]{2,1,0:T(1,128)} %broadcast_in_dim.5), calls=%async_computation.1 | async-start | bytes 196608 | tf_op jit(solution)/shard_map/all_to_all | solution.py:45
  263.7 6.8 %all-to-all-done.1 = f32[16,1,1536]{2,1,0:T(1,128)S(1)} async-done(((f32[16,1,1536]{2,1,0:T(1,128)}), f32[16,1,1536]{2,1,0:T(1,128)S(1)}, u32[]{:S(2)}, u32[]{:S(2)}) %all-to-all-start.1) | async-done | bytes 98336 | tf_op jit(solution)/shard_map/all_to_all | solution.py:45
  270.5 3.8 %all-to-all-start.3 = ((bf16[8,1,32]{2,1,0:T(2,128)(2,1)}), bf16[8,1,32]{2,1,0:T(2,128)(2,1)S(1)}, u32[]{:S(2)}, u32[]{:S(2)}) async-start(bf16[8,1,32]{2,1,0:T(2,128)(2,1)} %copy.66), calls=%async_computation.3 | async-start | bytes 8192 | tf_op jit(solution)/shard_map/all_to_all | solution.py:61
  274.4 14.3 %fusion.10 = bf16[4096,256]{0,1:T(8,128)(2,1)S(1)} fusion(bf16[4096,256]{0,1:T(8,128)(2,1)} %copy.55, f32[256,4096]{1,0:T(8,128)} %fusion.4, bf16[1,1,1536,4096]{3,2,1,0:T(8,128)(2,1)} %all-gather.20.cloned.1.call-done, bf16[1536,256]{0,1:T(8,128)(2,1)} %copy-done.3, f32[1536,256]{0,1:T(8,128)} %get-tuple-element.37, f32[1536]{0:T(1024)S(1)} %reduce_sum.160, ...), kind=kOutput, calls=%fused_computation.13 | convolution fusion | flops 3255566336 | bytes 23344128 | tf_op jit(solution)/shard_map/td,tf->df/dot_general | solution.py:105
  290.2 5.3 %all-to-all-start.2 = ((bf16[8,512,256]{1,2,0:T(8,128)(2,1)}), bf16[8,512,256]{1,2,0:T(8,128)(2,1)S(1)}, u32[]{:S(2)}, u32[]{:S(2)}) async-start(bf16[8,512,256]{1,2,0:T(8,128)(2,1)} %bitcast.114), calls=%async_computation.2 | async-start | bytes 4194304 | tf_op jit(solution)/shard_map/all_to_all | solution.py:61
  297.5 24.2 %all-to-all-done.2 = bf16[8,512,256]{1,2,0:T(8,128)(2,1)S(1)} async-done(((bf16[8,512,256]{1,2,0:T(8,128)(2,1)}), bf16[8,512,256]{1,2,0:T(8,128)(2,1)S(1)}, u32[]{:S(2)}, u32[]{:S(2)}) %all-to-all-start.2) | async-done | bytes 2097184 | tf_op jit(solution)/shard_map/all_to_all | solution.py:61
  (77 shorter events, 24.5 us)
Async XLA Ops:
  8.0 136.5 %all-reduce.3.cloned.1.call-start = ((), (), s32[]{:S(2)}) async-start(), calls=%async_computation.6 | async-start | bytes 4198400
  14.8 1.3 copy-start
  16.1 3.5 %copy-start.6 = (bf16[1,2,1536,256]{3,2,1,0:T(8,128)(2,1)S(1)}, bf16[1,2,1536,256]{3,2,1,0:T(8,128)(2,1)}, u32[]{:S(2)}) copy-start(bf16[1,2,1536,256]{3,2,1,0:T(8,128)(2,1)} %param.12) | copy-start | bytes 4718596
  16.1 142.1 %all-gather.18.cloned.1.call-start = ((), (), s32[]{:S(2)}) async-start(), calls=%async_computation.4 | async-start | bytes 13369344 | tf_op jit(solution)/shard_map/all_gather | solution.py:90
  19.0 203.5 %all-gather.20.cloned.1.call-start = ((), (), s32[]{:S(2)}) async-start(), calls=%async_computation.5 | async-start | bytes 13369344 | tf_op jit(solution)/shard_map/all_gather | solution.py:90
  193.8 2.1 copy-start.2
  195.9 0.9 copy-start.4
  197.5 14.0 %all-to-all-start = ((f32[16,1,1536]{2,1,0:T(1,128)}), f32[16,1,1536]{2,1,0:T(1,128)S(1)}, u32[]{:S(2)}, u32[]{:S(2)}) async-start(f32[16,1,1536]{2,1,0:T(1,128)} %broadcast_in_dim.4), calls=%async_computation | async-start | bytes 196608 | tf_op jit(solution)/shard_map/all_to_all | solution.py:45
  255.9 1.9 copy-start.1
  257.8 0.9 copy-start.3
  259.5 11.1 %all-to-all-start.1 = ((f32[16,1,1536]{2,1,0:T(1,128)}), f32[16,1,1536]{2,1,0:T(1,128)S(1)}, u32[]{:S(2)}, u32[]{:S(2)}) async-start(f32[16,1,1536]{2,1,0:T(1,128)} %broadcast_in_dim.5), calls=%async_computation.1 | async-start | bytes 196608 | tf_op jit(solution)/shard_map/all_to_all | solution.py:45
  270.5 19.7 %all-to-all-start.3 = ((bf16[8,1,32]{2,1,0:T(2,128)(2,1)}), bf16[8,1,32]{2,1,0:T(2,128)(2,1)S(1)}, u32[]{:S(2)}, u32[]{:S(2)}) async-start(bf16[8,1,32]{2,1,0:T(2,128)(2,1)} %copy.66), calls=%async_computation.3 | async-start | bytes 8192 | tf_op jit(solution)/shard_map/all_to_all | solution.py:61
  290.2 5.3 %copy-start.5 = (f32[512,256]{1,0:T(8,128)S(1)}, f32[512,256]{1,0:T(8,128)}, u32[]{:S(2)}) copy-start(f32[512,256]{1,0:T(8,128)} %param.7) | copy-start | bytes 1572868
  290.2 31.5 %all-to-all-start.2 = ((bf16[8,512,256]{1,2,0:T(8,128)(2,1)}), bf16[8,512,256]{1,2,0:T(8,128)(2,1)S(1)}, u32[]{:S(2)}, u32[]{:S(2)}) async-start(bf16[8,512,256]{1,2,0:T(8,128)(2,1)} %bitcast.114), calls=%async_computation.2 | async-start | bytes 4194304 | tf_op jit(solution)/shard_map/all_to_all | solution.py:61
  295.5 1.5 copy-start.7
  295.5 1.5 copy-start.8
Sparse Core Ops, SparseCore 0:
  16.2 128.2 all-reduce.2
Sparse Core Ops, SparseCore 1:
  19.1 95.1 all-gather.17
  116.5 88.6 all-gather.19
